TPU v7x, 32 devices: a whole 2x2x4 slice. The times are simulated.
32 devices in a mesh: date: 16 (over z, y, x), prod: 2 (over core).
Axes of the slice: x: 2, y: 2, z: 4, core: 2. Of those that a mesh axis runs over, the one named last changes fastest.
Arguments:
- daily_sales: float32 [256, 512, 128], P('prod', 'date'), may hold values from -2.5 to 2.5
- week_id: int32 [512], P('date'), may hold values from 0 to 102, never falling along the last dimension, each value on 1 to 7 neighbouring positions
- month_id: int32 [512], P('date'), may hold values from 0 to 21, never falling along the last dimension, each value on 1 to 31 neighbouring positions
- year_id: int32 [512], P('date'), may hold values from 0 to 1, never falling along the last dimension, each value on 1 to 366 neighbouring positions
Outputs:
- running: float32 [256, 512, 128], P('prod', 'date')
- week_total: float32 [256, 512, 128], P('prod', 'date')
- month_total: float32 [256, 512, 128], P('prod', 'date')
- year_total: float32 [256, 512, 128], P('prod', 'date')
- store_rollup: float32 [4, 512, 128], P(None, 'date')
Inputs may be any that keep to these rules, and one draw needn't show every extreme that they name: `week_id`: starts at 0 and never falls along the dates; each week covers 1 to 7 consecutive dates and some cover exactly 7. `month_id`: starts at 0 and never falls along the dates; each month covers 1 to 31 consecutive dates and some cover exactly 31; months need not line up with weeks. `year_id`: starts at 0 and never falls along the dates; each year covers 1 to 366 consecutive dates and some cover exactly 366; years need not line up with weeks or months.
All inputs are finite; a program needn't handle non-finite values.
Results may differ from a plain program's by a relative error of at most 0.000094.
Values sent between devices are 32-bit elements.
A program may use at most 64 MiB of HBM per device.

v0:
```python
import jax
import jax.numpy as jnp
from jax import lax
from jax.sharding import PartitionSpec as P

far_index = 1 << 30


def from_behind(block, axis, distance):
    devices = range(lax.axis_size(axis))
    route = [(i - distance, i) for i in devices if i - distance in devices]
    return lax.ppermute(block, axis, route)


def carried_in(value, axis, join, neutral, backward):
    count, mine = (lax.axis_size(axis), lax.axis_index(axis))
    pieces = jax.tree.map(lambda part: lax.all_gather(part, axis), value)
    if backward:
        pieces = jax.tree.map(lambda part: part[::-1], pieces)
        mine = count - 1 - mine
    running = jax.tree.map(
        lambda part, zero: jnp.full_like(part, 0) + jnp.asarray(zero, part.dtype), value, neutral
    )

    def step(position, running):
        longer = join(running, jax.tree.map(lambda part: part[position], pieces))
        return jax.tree.map(lambda new, old: jnp.where(position < mine, new, old), longer, running)

    return lax.fori_loop(0, count - 1, step, running)


def forward(earlier, latter):
    top_early, sums_early = earlier
    top_later, sums_later = latter
    inside = (top_later <= top_early)[:, None, None]
    return (jnp.maximum(top_early, top_later), sums_later + jnp.where(inside, sums_early, 0.0))


def backward(earlier, latter):
    low_early, sums_early = earlier
    low_later, sums_later = latter
    inside = (low_later >= low_early)[:, None, None]
    return (jnp.minimum(low_early, low_later), sums_later + jnp.where(inside, sums_early, 0.0))


def match_keep(ids_seen, ids_own, partial_value):
    return jnp.where((ids_seen == ids_own)[:, None, None], partial_value, 0.0)


def local(daily_sales, week_id, month_id, year_id):
    columns = daily_sales.shape[0]
    span_len = daily_sales.shape[1]
    level_ids = jnp.stack([jnp.zeros_like(week_id), week_id, month_id, year_id])
    offsets = lax.iota(jnp.int32, span_len)
    lower = (offsets[None, :] <= offsets[:, None]).astype(jnp.float32)
    matches = (level_ids[1:, :, None] == level_ids[1:, None, :]).astype(jnp.float32)
    mixers = jnp.concatenate([lower[None], matches], axis=0)
    within = jnp.einsum("kij,pjs->kpis", mixers, daily_sales, precision=lax.Precision.HIGHEST)
    tail_sums = within[:, :, -1, :]
    head_sums = within[1:, :, 0, :]
    first_ids = level_ids[:, 0]
    last_ids = level_ids[:, -1]
    left_ids, left_sums = from_behind((last_ids[1:3], tail_sums[1:3]), "date", 1)
    right_ids, right_sums = from_behind((first_ids[1:3], head_sums[0:2]), "date", -1)
    outer_ids = jnp.stack([last_ids[0], last_ids[3]])
    outer_sums = jnp.stack([tail_sums[0], tail_sums[3]])
    start = (jnp.full((2,), -1, jnp.int32), jnp.zeros_like(outer_sums))
    top_prev, sums_prev = carried_in((outer_ids, outer_sums), "date", forward, start, False)
    outer_in = match_keep(top_prev, jnp.stack([first_ids[0], first_ids[3]]), sums_prev)
    finish = (jnp.full((1,), far_index, jnp.int32), jnp.zeros_like(head_sums[2:]))
    low_next, sums_next = carried_in((first_ids[3:], head_sums[2:]), "date", backward, finish, True)
    middle_in = match_keep(left_ids, first_ids[1:3], left_sums)
    carry_in = jnp.concatenate([outer_in[:1], middle_in, outer_in[1:]], axis=0)
    middle_back = match_keep(right_ids, last_ids[1:3], right_sums)
    carry_back = jnp.concatenate(
        [middle_back, match_keep(low_next, last_ids[3:], sums_next)], axis=0
    )
    start_gain = (level_ids[1:] == first_ids[1:, None]).astype(jnp.float32)
    end_gain = (level_ids[1:] == last_ids[1:, None]).astype(jnp.float32)
    running = within[0] + carry_in[0][:, None, :]
    levels = (
        within[1:]
        + carry_in[1:, :, None, :] * start_gain[:, None, :, None]
        + carry_back[:, :, None, :] * end_gain[:, None, :, None]
    )
    product_terms = jnp.concatenate(
        [jnp.sum(running, axis=0)[None], jnp.sum(levels, axis=1)], axis=0
    )
    store_rollup = lax.psum(product_terms, "prod")
    return (running, levels[0, :columns], levels[1, :columns], levels[2, :columns], store_rollup)


def solution(mesh):
    return jax.shard_map(
        local,
        mesh=mesh,
        in_specs=(P("prod", "date", None), P("date"), P("date"), P("date")),
        out_specs=(
            P("prod", "date", None),
            P("prod", "date", None),
            P("prod", "date", None),
            P("prod", "date", None),
            P(None, "date", None),
        ),
        check_vma=False,
    )
```

profile of v0, /device:TPU:0, one launch (start us, length us, event | category | flops | bytes accessed | tf_op | source)
XLA Modules:
  0.0 187.9 jit_solution(4630445050261132228)
XLA Ops:
  8.9 3.4 %convolution_bitcast_fusion = f32[4,128,32,128]{3,2,1,0:T(8,128)S(1)} fusion(f32[128,32,128]{2,1,0:T(8,128)S(1)} %copy-done, pred[3,32,32]{2,1,0:T(32,128)(4,1)S(1)} %broadcast_compare_fusion, pred[1,32,32]{2,1,0:T(32,128)(4,1)S(1)} %iota_compare_fusion), kind=kOutput, calls=%fused_computation.11 | convolution fusion | flops 805310464 | bytes 10489856 | tf_op jit(solution)/shard_map/kij,pjs->kpis/dot_general | solution.py:58
  12.3 3.2 %copy-done.1 = f32[4,128,32,128]{3,2,1,0:T(8,128)} copy-done((f32[4,128,32,128]{3,2,1,0:T(8,128)}, f32[4,128,32,128]{3,2,1,0:T(8,128)S(1)}, u32[]{:S(2)}) %copy-start.1) | copy-done | bytes 8388632
  16.6 4.9 %collective-permute-start = (s32[2]{0:T(128)S(1)}, s32[2]{0:T(128)S(1)}, u32[]{:S(2)}, u32[]{:S(2)}) collective-permute-start(s32[2]{0:T(128)S(1)} %get-tuple-element.291), channel_id=1, source_target_pairs={{0,2},{2,4},{4,6},{6,8},{8,10},{10,12},{12,14},{14,16},{16,18},{18... | collective-permute-start | bytes 32 | tf_op jit(solution)/shard_map/ppermute | solution.py:12
  21.5 1.7 fusion.12
  23.2 3.4 %collective-permute-start.1 = (f32[2,128,128]{2,1,0:T(8,128)S(1)}, f32[2,128,128]{2,1,0:T(8,128)S(1)}, u32[]{:S(2)}, u32[]{:S(2)}) collective-permute-start(f32[2,128,128]{2,1,0:T(8,128)S(1)} %bitcast.81), channel_id=1, source_target_pairs={{0,2},{2,4},{4,6},{6,8},{8,10},{10,12},{12,14},{14,16},{16,18},{18... | collective-permute-start | bytes 393224 | tf_op jit(solution)/shard_map/ppermute | solution.py:12
  26.6 1.3 collective-permute-start.2
  27.9 1.3 collective-permute-start.3
  32.8 1.4 bitcast_dynamic-update-slice_fusion
  34.1 17.9 %all-reduce.3 = (s32[32]{0:T(128)S(1)}, s32[16]{0:T(128)S(1)}) all-reduce(s32[32]{0:T(128)S(1)} %pad_dynamic-update-slice_fusion, s32[16]{0:T(128)S(1)} %bitcast_dynamic-update-slice_fusion), channel_id=2, replica_groups=mesh['date'=16,'prod'=2] {'date'}, use_global_device_ids=true, to_apply=%add.1 | all-reduce | flops 48 | bytes 384
  53.2 21.4 %all-gather.8.cloned.1.call-done = f32[16,128,1,128]{3,1,2,0:T(8,128)} async-done(((f32[1,128,1,128]{3,1,2,0:T(8,128)}), f32[16,128,1,128]{3,1,2,0:T(8,128)}) %all-gather.8.cloned.1.call-update) | async-done | bytes 1048592 | tf_op jit(solution)/shard_map/all_gather | solution.py:17
  74.6 1.3 reverse_bitcast_fusion
  75.9 28.3 %while.33 = (s32[]{:T(128)}, s32[1]{0:T(128)}, f32[1,128,128]{2,1,0:T(8,128)S(1)}, s32[]{:T(128)}, s32[16,1]{0,1:T(1,128)S(1)}, /*index=5*/f32[16,1,128,128]{3,2,1,0:T(8,128)S(1)}, s32[]{:T(128)}, s32[]{:T(128)}) while((s32[]{:T(128)}, s32[1]{0:T(128)}, f32[1,128,128]{2,1,0:T(8,128)S(1)}, s32[]{:T(128)}, s32[16,1]{0,1:T(1,128)S(1)}, ...), condition=%wide.region_3.4_spmd.clone, body=%wide.region_2.3_spmd.clone.sunk | while | flops 65543 | bytes 196764 | solution.py:29
  105.7 31.5 %all-gather.6.cloned.1.call-done = f32[32,128,128]{2,1,0:T(8,128)} async-done(((f32[2,128,128]{2,1,0:T(8,128)}), f32[32,128,128]{2,1,0:T(8,128)}) %all-gather.6.cloned.1.call-update) | async-done | bytes 2097168 | tf_op jit(solution)/shard_map/all_gather | solution.py:17
  137.3 15.9 %while.32 = (s32[]{:T(128)}, s32[2]{0:T(128)S(1)}, f32[2,128,128]{2,1,0:T(8,128)S(1)}, s32[]{:T(128)}, s32[16,2]{1,0:T(8,128)S(1)}, /*index=5*/f32[16,2,128,128]{3,2,1,0:T(8,128)}, s32[]{:T(128)}, s32[]{:T(128)}) while((s32[]{:T(128)}, s32[2]{0:T(128)S(1)}, f32[2,128,128]{2,1,0:T(8,128)S(1)}, s32[]{:T(128)}, ...), condition=%wide.region_1.2_spmd.clone, body=%wide.region_0.1_spmd.clone.sunk | while | flops 131086 | bytes 393380 | solution.py:29
  137.3 1.0 fusion.18
  138.4 1.0 fusion.18
  139.4 1.0 fusion.18
  140.5 1.0 fusion.18
  141.5 1.0 fusion.18
  154.1 3.2 %fusion.8 = (f32[32,128]{1,0:T(8,128)S(1)}, f32[128,32,128]{2,1,0:T(8,128)}) fusion(f32[128,128]{1,0:T(8,128)S(1)} %get-tuple-element.332, f32[4,128,32,128]{3,2,1,0:T(8,128)} %copy-done.1), kind=kLoop, calls=%fused_computation.45 | loop fusion | flops 1044480 | bytes 4276224 | tf_op jit(solution)/shard_map/reduce_sum | solution.py:87
  157.3 5.3 %fusion.10 = (f32[3,32,128]{2,1,0:T(8,128)S(1)}, f32[3,128,32,128]{3,2,1,0:T(8,128)}) fusion(f32[3,32]{1,0:T(4,128)S(1)} %get-tuple-element.334, f32[3,128,128]{2,1,0:T(8,128)S(1)} %pad_maximum_fusion.1, f32[3,32]{1,0:T(4,128)S(1)} %get-tuple-element.333, f32[3,128,128]{2,1,0:T(8,128)S(1)} %pad_maximum_fusion, f32[4,128,32,128]{3,2,1,0:T(8,128)} %copy-done.1), kind=kLoop, calls=%fused_computation.46 | loop fusion | flops 7852032 | bytes 13026048 | tf_op jit(solution)/shard_map/reduce_sum | solution.py:87
  163.2 5.7 %slice_bitcast_fusion = (f32[128,32,128]{2,1,0:T(8,128)}, f32[128,32,128]{2,1,0:T(8,128)}, f32[128,32,128]{2,1,0:T(8,128)}) fusion(f32[3,128,32,128]{3,2,1,0:T(8,128)} %get-tuple-element.322), kind=kLoop, calls=%fused_computation.12 | loop fusion | bytes 12582912 | tf_op jit(solution)/shard_map/squeeze | solution.py:90
  168.9 10.9 %all-reduce.6.cloned.1.call-done = f32[4,32,128]{2,1,0:T(8,128)} async-done(((f32[4,32,128]{2,1,0:T(8,128)}), f32[4,32,128]{2,1,0:T(8,128)}) %all-reduce.6.cloned.1.call-update) | async-done | bytes 65552 | tf_op jit(solution)/shard_map/psum | solution.py:89
  179.9 1.5 copy.49
  (121 shorter events, 28.6 us)
Async XLA Ops:
  7.2 1.7 copy-start
  7.2 23.6 %copy-start.5 = (u32[32]{0:T(128)S(1)}, u32[32]{0:T(128)}, u32[]{:S(2)}) copy-start(u32[32]{0:T(128)} %constant.81) | copy-start | bytes 388
  7.2 9.2 %copy-start.4 = (s32[32]{0:T(128)S(1)}, s32[32]{0:T(128)}, u32[]{:S(2)}) copy-start(s32[32]{0:T(128)} %param.9) | copy-start | bytes 388
  7.2 9.2 %copy-start.3 = (s32[32]{0:T(128)S(1)}, s32[32]{0:T(128)}, u32[]{:S(2)}) copy-start(s32[32]{0:T(128)} %param.10) | copy-start | bytes 388
  7.2 22.8 %copy-start.2 = (s32[32]{0:T(128)S(1)}, s32[32]{0:T(128)}, u32[]{:S(2)}) copy-start(s32[32]{0:T(128)} %param.11) | copy-start | bytes 388
  7.2 67.4 %all-gather.8.cloned.1.call-start = ((), (), s32[]{:S(2)}) async-start(), calls=%async_computation.2 | async-start | bytes 1114112 | tf_op jit(solution)/shard_map/all_gather | solution.py:17
  12.3 3.2 %copy-start.1 = (f32[4,128,32,128]{3,2,1,0:T(8,128)}, f32[4,128,32,128]{3,2,1,0:T(8,128)S(1)}, u32[]{:S(2)}) copy-start(f32[4,128,32,128]{3,2,1,0:T(8,128)S(1)} %convolution_bitcast_fusion) | copy-start | bytes 25165828
  16.3 120.9 %all-gather.6.cloned.1.call-start = ((), (), s32[]{:S(2)}) async-start(), calls=%async_computation.1 | async-start | bytes 2228224 | tf_op jit(solution)/shard_map/all_gather | solution.py:17
  16.6 35.7 %collective-permute-start = (s32[2]{0:T(128)S(1)}, s32[2]{0:T(128)S(1)}, u32[]{:S(2)}, u32[]{:S(2)}) collective-permute-start(s32[2]{0:T(128)S(1)} %get-tuple-element.291), channel_id=1, source_target_pairs={{0,2},{2,4},{4,6},{6,8},{8,10},{10,12},{12,14},{14,16},{16,18},{18... | collective-permute-start | bytes 32 | tf_op jit(solution)/shard_map/ppermute | solution.py:12
  23.2 29.2 %collective-permute-start.1 = (f32[2,128,128]{2,1,0:T(8,128)S(1)}, f32[2,128,128]{2,1,0:T(8,128)S(1)}, u32[]{:S(2)}, u32[]{:S(2)}) collective-permute-start(f32[2,128,128]{2,1,0:T(8,128)S(1)} %bitcast.81), channel_id=1, source_target_pairs={{0,2},{2,4},{4,6},{6,8},{8,10},{10,12},{12,14},{14,16},{16,18},{18... | collective-permute-start | bytes 393224 | tf_op jit(solution)/shard_map/ppermute | solution.py:12
  26.6 25.7 %collective-permute-start.2 = (s32[2]{0:T(128)S(1)}, s32[2]{0:T(128)S(1)}, u32[]{:S(2)}, u32[]{:S(2)}) collective-permute-start(s32[2]{0:T(128)S(1)} %get-tuple-element.292), channel_id=1, source_target_pairs={{2,0},{4,2},{6,4},{8,6},{10,8},{12,10},{14,12},{16,14},{18,16},{20... | collective-permute-start | bytes 32 | tf_op jit(solution)/shard_map/ppermute | solution.py:12
  27.9 24.5 %collective-permute-start.3 = (f32[2,128,128]{2,1,0:T(8,128)S(1)}, f32[2,128,128]{2,1,0:T(8,128)S(1)}, u32[]{:S(2)}, u32[]{:S(2)}) collective-permute-start(f32[2,128,128]{2,1,0:T(8,128)S(1)} %bitcast.80), channel_id=1, source_target_pairs={{2,0},{4,2},{6,4},{8,6},{10,8},{12,10},{14,12},{16,14},{18,16},{20... | collective-permute-start | bytes 393224 | tf_op jit(solution)/shard_map/ppermute | solution.py:12
  29.9 149.9 %all-reduce.6.cloned.1.call-start = ((), (), s32[]{:S(2)}) async-start(), calls=%async_computation | async-start | bytes 131072 | tf_op jit(solution)/shard_map/psum | solution.py:89
Sparse Core Ops, SparseCore 0:
  16.5 58.0 all-gather.7
  77.9 59.2 all-gather.5
  163.3 16.4 all-reduce.5
where the time goes:
time: 189 us; the launch traced here: 188 us
  waiting for transfers between devices  63.9 us (34%)
  other arithmetic  29.1 us (15%)
  local copies, waits for them, and re-layouts  27.6 us (15%)
  loops' own time  19.6 us (10%)
  blocking collectives  17.9 us (9%)
  between operations  15.2 us (8%)
  starting transfers between devices  11 us (6%)
  matrix products  3.44 us (2%)
    all_gather x2, waiting for transfers between devices, carried_in(): pieces = jax.tree.map(lambda part: lax.all_gather(part, axis), value)  52.9 us
    another operation x2, loops' own time, carried_in(): return lax.fori_loop(0, count - 1, step, running)  19.6 us
    unnamed x1, blocking collectives  17.9 us
    select_n x45, other arithmetic, step(): jnp.where(position < mine, new, old)  15.5 us
    psum x1, waiting for transfers between devices, local(): store_rollup = lax.psum(product_terms, 'prod')  10.9 us
    ppermute x4, starting transfers between devices, from_behind(): return lax.ppermute(block, axis, route)  10.9 us
    unnamed x20, local copies, waits for them, and re-layouts  9.45 us
    dynamic_slice x15, local copies, waits for them, and re-layouts, step(): longer = join(running, jax.tree.map(lambda part: part[position], pieces))  8.89 us
  transfers between devices with their start and end apart: 7, of which 3 were waited for; matrix products, arithmetic and copies ran while one was open for 13% of the time, Pallas kernels for 0%

commit v1 on v0

v1 whole, which is shorter than its diff:
```python
import functools

import jax
import jax.numpy as jnp
from jax import lax
from jax.experimental import pallas as pl
from jax.experimental.pallas import tpu as pltpu
from jax.sharding import PartitionSpec as P

MESH = pl.DeviceIdType.MESH
F32 = jnp.float32


def id_column(ids, span, lanes):
    where = lax.broadcasted_iota(jnp.int32, (span, lanes), 0)
    column = jnp.zeros((span, lanes), jnp.int32)
    for t in range(span):
        column = jnp.where(where == t, ids[t], column)
    return column


def id_row(ids, span, lanes):
    where = lax.broadcasted_iota(jnp.int32, (span, lanes), 1) % span
    row = jnp.zeros((span, lanes), jnp.int32)
    for t in range(span):
        row = jnp.where(where == t, ids[t], row)
    return row


def edge_masks(ids, span, lanes):
    column = id_column(ids, span, lanes)
    return (column == ids[0]).astype(F32), (column == ids[span - 1]).astype(F32)


def stack_rows(values, rows, lanes):
    where = lax.broadcasted_iota(jnp.int32, (rows, lanes), 0)
    tile = jnp.zeros((rows, lanes), F32)
    for i, value in enumerate(values):
        tile = jnp.where(where == i, value, tile)
    return tile


def exchange_kernel(
    n, n_prod, slices, loads,
    week, month, year, x_hbm,
    carry, near, meta,
    x, send1, recv1, send2, edges, sib,
    load_sem, s1_sem, r1_sem, s2_sem, r2_sem, sib_s, sib_r, near_s, near_r,
):
    me = lax.axis_index("date")
    core = lax.axis_index("prod")
    columns, span, lanes = x.shape
    rows = columns // slices
    chunk = columns // loads
    loaded = [
        pltpu.make_async_copy(
            x_hbm.at[pl.ds(i * chunk, chunk)], x.at[pl.ds(i * chunk, chunk)], load_sem.at[i]
        )
        for i in range(loads)
    ]
    for copy in loaded:
        copy.start()
    barrier = pltpu.get_barrier_semaphore()
    for d in range(1, n):
        pl.semaphore_signal(
            barrier, inc=1, device_id=(lax.rem(me + d, n), core), device_id_type=MESH
        )
    for d in range(1, n_prod):
        pl.semaphore_signal(
            barrier, inc=1, device_id=(me, lax.rem(core + d, n_prod)), device_id_type=MESH
        )
    head_y, tail_y = edge_masks(year, span, lanes)
    last = span - 1
    ids = stack_rows(
        [
            v.astype(F32)
            for v in (year[0], year[last], week[0], week[last], month[0], month[last])
        ],
        rows, lanes,
    )

    def outer_sums(s, total):
        block = x[pl.ds(pl.multiple_of(s * rows, rows), rows)]
        send1[s, 0] = jnp.sum(block, axis=1)
        send1[s, 1] = jnp.sum(block * head_y[None], axis=1)
        send1[s, 2] = jnp.sum(block * tail_y[None], axis=1)
        send1[s, 3] = ids
        return total + jnp.sum(block, axis=0)

    total = jnp.zeros((span, lanes), F32)
    per_load = slices // loads
    for i in range(loads):
        loaded[i].wait()
        total = lax.fori_loop(i * per_load, (i + 1) * per_load, outer_sums, total)
    sib[core] = total
    pl.semaphore_wait(barrier, n - 1 + n_prod - 1)

    first = []
    for d in range(1, n):
        peer = lax.rem(me + d, n)
        copy = pltpu.make_async_remote_copy(
            src_ref=send1.at[lax.rem(peer, slices)], dst_ref=recv1.at[me],
            send_sem=s1_sem.at[peer], recv_sem=r1_sem.at[me],
            device_id=(peer, core), device_id_type=MESH,
        )
        copy.start()
        first.append(copy)
    shared = []
    for d in range(1, n_prod):
        peer = lax.rem(core + d, n_prod)
        copy = pltpu.make_async_remote_copy(
            src_ref=sib.at[core], dst_ref=sib.at[core],
            send_sem=sib_s.at[peer], recv_sem=sib_r.at[core],
            device_id=(me, peer), device_id_type=MESH,
        )
        copy.start()
        shared.append(copy)

    head_w, tail_w = edge_masks(week, span, lanes)
    head_m, tail_m = edge_masks(month, span, lanes)

    def inner_sums(s, nothing):
        at = pl.ds(pl.multiple_of(s * rows, rows), rows)
        block = x[at]
        edges[0, 0, at] = jnp.sum(block * tail_w[None], axis=1)
        edges[0, 1, at] = jnp.sum(block * tail_m[None], axis=1)
        edges[1, 0, at] = jnp.sum(block * head_w[None], axis=1)
        edges[1, 1, at] = jnp.sum(block * head_m[None], axis=1)
        return nothing

    lax.fori_loop(0, slices, inner_sums, 0)
    left, right = lax.rem(me + n - 1, n), lax.rem(me + 1, n)
    beside = []
    for side, peer in ((0, right), (1, left)):
        copy = pltpu.make_async_remote_copy(
            src_ref=edges.at[side], dst_ref=near.at[side],
            send_sem=near_s.at[side], recv_sem=near_r.at[side],
            device_id=(peer, core), device_id_type=MESH,
        )
        copy.start()
        beside.append(copy)

    recv1[me] = send1[lax.rem(me, slices)]
    for d in range(1, n_prod):
        peer = lax.rem(core + d, n_prod)
        pltpu.make_async_remote_copy(
            src_ref=sib.at[core], dst_ref=sib.at[peer],
            send_sem=sib_s.at[peer], recv_sem=sib_r.at[peer],
            device_id=(me, peer), device_id_type=MESH,
        ).wait_recv()
    whole = sib[0]
    for i in range(1, n_prod):
        whole = whole + sib[i]
    sums = stack_rows(
        [
            jnp.sum(whole * m, axis=0, keepdims=True)
            for m in (jnp.ones_like(head_y), head_y, tail_y, head_w, tail_w, head_m, tail_m)
        ],
        rows, lanes,
    )

    def arrived(buffer, send_sem, recv_sem):
        for d in range(1, n):
            peer = lax.rem(me + d, n)
            pltpu.make_async_remote_copy(
                src_ref=send1.at[0], dst_ref=buffer.at[peer],
                send_sem=send_sem.at[peer], recv_sem=recv_sem.at[peer],
                device_id=(peer, core), device_id_type=MESH,
            ).wait_recv()

    arrived(recv1, s1_sem, r1_sem)
    low = [recv1[b, 3, 0:1, :] for b in range(n)]
    top = [recv1[b, 3, 1:2, :] for b in range(n)]
    running = jnp.zeros((rows, lanes), F32)
    into = jnp.zeros((rows, lanes), F32)
    for b in range(n):
        send2[b, 0] = running
        send2[b, 1] = into
        send2[b, 3] = sums
        if b + 1 < n:
            running = running + recv1[b, 0]
            held = recv1[b, 2] + jnp.where(low[b] == top[b], into, 0.0)
            into = jnp.where(top[b] == low[b + 1], held, 0.0)
    back = jnp.zeros((rows, lanes), F32)
    for b in reversed(range(n)):
        send2[b, 2] = back
        if b > 0:
            held = recv1[b, 1] + jnp.where(low[b] == top[b], back, 0.0)
            back = jnp.where(top[b - 1] == low[b], held, 0.0)

    second = []
    for d in range(1, n):
        peer = lax.rem(me + d, n)
        copy = pltpu.make_async_remote_copy(
            src_ref=send2.at[peer], dst_ref=carry.at[me],
            send_sem=s2_sem.at[peer], recv_sem=r2_sem.at[me],
            device_id=(peer, core), device_id_type=MESH,
        )
        copy.start()
        second.append(copy)
    carry[me] = send2[me]
    arrived(carry, s2_sem, r2_sem)

    zero = jnp.zeros((1, lanes), F32)
    run_sum, in_sum, back_sum = zero, zero, zero
    low_me, top_me = year[0].astype(F32), year[last].astype(F32)
    for b in range(n):
        tile = carry[b, 3]
        run_sum = run_sum + jnp.where(b < me, tile[0:1], 0.0)
        inside = jnp.logical_and(top[b] == low_me, b < me)
        in_sum = in_sum + jnp.where(inside, tile[2:3], 0.0)
        inside = jnp.logical_and(low[b] == top_me, b > me)
        back_sum = back_sum + jnp.where(inside, tile[1:2], 0.0)
    left_ids, right_ids = recv1[left, 3], recv1[right, 3]
    left_sums, right_sums = carry[left, 3], carry[right, 3]

    def gain(seen, own, there):
        return jnp.where(jnp.logical_and(seen == own.astype(F32), there), 1.0, 0.0)

    week_l = gain(left_ids[3:4], week[0], me > 0)
    month_l = gain(left_ids[5:6], month[0], me > 0)
    week_r = gain(right_ids[2:3], week[last], me < n - 1)
    month_r = gain(right_ids[4:5], month[last], me < n - 1)
    meta[0:8] = stack_rows(
        [
            run_sum, in_sum, back_sum,
            left_sums[4:5] * week_l, left_sums[6:7] * month_l,
            right_sums[3:4] * week_r, right_sums[5:6] * month_r,
        ],
        8, lanes,
    )
    meta[8:16] = stack_rows([week_l, month_l, week_r, month_r], 8, lanes)
    meta[16 : 16 + span] = whole
    for copy in beside:
        copy.wait()
    for copy in first + shared + second:
        copy.wait_send()


def exchange(n, n_prod, slices, week, month, year, sales):
    columns, span, lanes = sales.shape
    rows = columns // slices
    loads = 4 if slices % 4 == 0 else 1
    smem = pl.BlockSpec(memory_space=pltpu.SMEM)
    vmem = pl.BlockSpec(memory_space=pltpu.VMEM)
    anywhere = pl.BlockSpec(memory_space=pl.ANY)
    packet = (n, 4, rows, lanes)
    dma = pltpu.SemaphoreType.DMA
    return pl.pallas_call(
        functools.partial(exchange_kernel, n, n_prod, slices, loads),
        out_shape=(
            jax.ShapeDtypeStruct(packet, F32),
            jax.ShapeDtypeStruct((2, 2, columns, lanes), F32),
            jax.ShapeDtypeStruct((16 + span, lanes), F32),
        ),
        in_specs=[smem, smem, smem, anywhere],
        out_specs=(vmem, anywhere, vmem),
        scratch_shapes=[
            pltpu.VMEM(sales.shape, F32),
            pltpu.VMEM((slices, 4, rows, lanes), F32),
            pltpu.VMEM(packet, F32),
            pltpu.VMEM(packet, F32),
            pltpu.VMEM((2, 2, columns, lanes), F32),
            pltpu.VMEM((n_prod, span, lanes), F32),
            dma((loads,)), dma((n,)), dma((n,)), dma((n,)), dma((n,)),
            dma((n_prod,)), dma((n_prod,)), dma((2,)), dma((2,)),
        ],
        compiler_params=pltpu.CompilerParams(collective_id=0, has_side_effects=True),
        name="exchange",
    )(week, month, year, sales)


def split3(value):
    high = value.astype(jnp.bfloat16)
    rest = value - high.astype(F32)
    middle = rest.astype(jnp.bfloat16)
    low = (rest - middle.astype(F32)).astype(jnp.bfloat16)
    return jnp.concatenate([high, middle, low], axis=-2)


def apply_kernel(
    week, month, year, x, carry, near, meta,
    run_out, week_out, month_out, year_out, rollup,
    mixer, gains,
):
    _, span, lanes = x.shape
    groups, _, rows, _ = carry.shape

    @pl.when(pl.program_id(0) == 0)
    def _():
        sub = lax.broadcasted_iota(jnp.int32, (span, 3 * span), 0)
        lane = lax.broadcasted_iota(jnp.int32, (span, 3 * span), 1) % span
        mixer[0:span] = jnp.where(lane <= sub, 1.0, 0.0).astype(mixer.dtype)
        for k, ids in enumerate((week, month, year)):
            same = id_column(ids, span, 3 * span) == id_row(ids, span, 3 * span)
            mixer[(k + 1) * span : (k + 2) * span] = jnp.where(same, 1.0, 0.0).astype(mixer.dtype)
            head, tail = edge_masks(ids, span, lanes)
            if k == 0:
                sum_head, sum_tail = head, tail
            gains[2 * k] = head
            gains[2 * k + 1] = tail
        mixed = jnp.dot(mixer[...], split3(meta[16 : 16 + span]), preferred_element_type=F32)
        rollup[0] = mixed[0:span] + meta[0:1]
        rollup[1] = mixed[span : 2 * span] + meta[3:4] * gains[0] + meta[5:6] * gains[1]
        rollup[2] = mixed[2 * span : 3 * span] + meta[4:5] * gains[2] + meta[6:7] * gains[3]
        rollup[3] = mixed[3 * span : 4 * span] + meta[1:2] * gains[4] + meta[2:3] * gains[5]
        gains[0] = gains[0] * meta[8:9]
        gains[1] = gains[1] * meta[10:11]
        gains[2] = gains[2] * meta[9:10]
        gains[3] = gains[3] * meta[11:12]

    def group(g, nothing):
        base = pl.multiple_of(g * rows, rows)
        at = pl.ds(base, rows)
        left_w, left_m = near[0, 0, at], near[0, 1, at]
        right_w, right_m = near[1, 0, at], near[1, 1, at]
        start, year_l, year_r = carry[g, 0], carry[g, 1], carry[g, 2]
        for r in range(0, rows, 2):
            parts = split3(x[pl.ds(base + r, 2)])
            both = jnp.concatenate([parts[0], parts[1]], axis=1)
            mixed = jnp.dot(mixer[...], both, preferred_element_type=F32)
            for j in range(2):
                q = r + j
                row = slice(q, q + 1)
                own = mixed[:, j * lanes : (j + 1) * lanes]
                run_out[base + q] = own[0:span] + start[row]
                week_out[base + q] = (
                    own[span : 2 * span] + left_w[row] * gains[0] + right_w[row] * gains[1]
                )
                month_out[base + q] = (
                    own[2 * span : 3 * span] + left_m[row] * gains[2] + right_m[row] * gains[3]
                )
                year_out[base + q] = (
                    own[3 * span : 4 * span] + year_l[row] * gains[4] + year_r[row] * gains[5]
                )
        return nothing

    lax.fori_loop(0, groups, group, 0)


def apply(slices, week, month, year, sales, carry, near, meta):
    columns, span, lanes = sales.shape
    rows = columns // slices
    steps = 8 if slices % 8 == 0 else 1
    block = columns // steps
    smem = pl.BlockSpec(memory_space=pltpu.SMEM)
    cube = pl.BlockSpec((block, span, lanes), lambda i: (i, 0, 0))
    cube_shape = jax.ShapeDtypeStruct(sales.shape, F32)
    return pl.pallas_call(
        apply_kernel,
        grid=(steps,),
        out_shape=(cube_shape,) * 4 + (jax.ShapeDtypeStruct((4, span, lanes), F32),),
        in_specs=[
            smem, smem, smem, cube,
            pl.BlockSpec((slices // steps, 4, rows, lanes), lambda i: (i, 0, 0, 0)),
            pl.BlockSpec((2, 2, block, lanes), lambda i: (0, 0, i, 0)),
            pl.BlockSpec(meta.shape, lambda i: (0, 0)),
        ],
        out_specs=(cube,) * 4 + (pl.BlockSpec((4, span, lanes), lambda i: (0, 0, 0)),),
        scratch_shapes=[
            pltpu.VMEM((4 * span, 3 * span), jnp.bfloat16),
            pltpu.VMEM((6, span, lanes), F32),
        ],
        compiler_params=pltpu.CompilerParams(dimension_semantics=("arbitrary",)),
        name="apply",
    )(week, month, year, sales, carry, near, meta)


def solution(mesh):
    n, n_prod = mesh.shape["date"], mesh.shape["prod"]

    def local(sales, week, month, year):
        slices = min(n, sales.shape[0] // 8)
        carry, near, meta = exchange(n, n_prod, slices, week, month, year, sales)
        return apply(slices, week, month, year, sales, carry, near, meta)

    return jax.shard_map(
        local,
        mesh=mesh,
        in_specs=(P("prod", "date", None), P("date"), P("date"), P("date")),
        out_specs=(P("prod", "date", None),) * 4 + (P(None, "date", None),),
        check_vma=False,
    )
```

time: 189 us -> 35.4 us (0.19)
  waiting for transfers between devices: 63.9 us -> 0 us
  Pallas kernels: 0 us -> 34.5 us
  other arithmetic: 29.1 us -> 0 us
  local copies, waits for them, and re-layouts: 27.6 us -> 0 us
  loops' own time: 19.6 us -> 0 us
  blocking collectives: 17.9 us -> 0 us
  between operations: 15.2 us -> 0.64 us
  starting transfers between devices: 11 us -> 0 us
  matrix products: 3.44 us -> 0 us
    all_gather x2 -> x0, waiting for transfers between devices: 52.9 us -> none  [carried_in(): pieces = jax.tree.map(lambda part: lax.all_gather(part, axis), value)]
    pallas_call x0 -> x2, Pallas kernels: none -> 34.5 us  [the longest x1 26 us: exchange(): pl.pallas_call(functools.partial(exchange_kernel, n, n_prod, slices, load...]
    another operation x2 -> x0, loops' own time: 19.6 us -> none  [carried_in(): return lax.fori_loop(0, count - 1, step, running)]
    unnamed x1 -> x0, blocking collectives: 17.9 us -> none
    select_n x49 -> x0, other arithmetic: 16.4 us -> none  [the longest x45 15.5 us: step(): jnp.where(position < mine, new, old)]
    psum x1 -> x0, waiting for transfers between devices: 10.9 us -> none  [local(): store_rollup = lax.psum(product_terms, 'prod')]
    ppermute x4 -> x0, starting transfers between devices: 10.9 us -> none  [from_behind(): return lax.ppermute(block, axis, route)]
    unnamed x20 -> x0, local copies, waits for them, and re-layouts: 9.45 us -> none
  transfers between devices with their start and end apart: 7 -> 0, of which waited for: 3 -> 0; matrix products, arithmetic and copies ran while one was open for 13% -> 0% of each run, Pallas kernels for 0% -> 0%
where the time goes in v1:
time: 35.4 us; the launch traced here: 35.1 us
  Pallas kernels  34.5 us (97%)
  between operations  0.64 us (2%)
    pallas_call x1, Pallas kernels, exchange(): pl.pallas_call(functools.partial(exchange_kernel, n, n_prod, slices, load...  26 us
    pallas_call x1, Pallas kernels, apply(): pl.pallas_call(apply_kernel, grid=(steps,), out_shape=(cube_shape,) * 4 +...  8.48 us

profile of v1, /device:TPU:0, one launch (start us, length us, event | category | flops | bytes accessed | tf_op | source)
XLA Modules:
  0.0 35.1 jit_solution(12481168873961498348)
XLA Ops:
  0.6 26.0 %exchange.1 = (f32[16,4,8,128]{3,2,1,0:T(8,128)}, f32[2,2,128,128]{3,2,1,0:T(8,128)}, f32[48,128]{1,0:T(8,128)}) custom-call(s32[32]{0:T(128)} %week.3, s32[32]{0:T(128)} %month.3, s32[32]{0:T(128)} %year.3, f32[128,32,128]{2,1,0:T(8,128)} %x.1), custom_call_target="tpu_custom_call" | custom-call | tf_op jit(solution)/shard_map/exchange/pallas_call | solution.py:249
  26.7 8.5 %apply.1 = (f32[128,32,128]{2,1,0:T(8,128)}, f32[128,32,128]{2,1,0:T(8,128)}, f32[128,32,128]{2,1,0:T(8,128)}, f32[128,32,128]{2,1,0:T(8,128)}, f32[4,32,128]{2,1,0:T(8,128)}) custom-call(s32[32]{0:T(128)} %week.3, s32[32]{0:T(128)} %month.3, s32[32]{0:T(128)} %year.3, f32[128,32,128]{2,1,0:T(8,128)} %x.1, f32[16,4,8,128]{3,2,1,0:T(8,128)} %get-tuple-element.8.carry, ...), custom_call_target="tpu_custom_call" | custom-call | tf_op jit(solution)/shard_map/apply/pallas_call | solution.py:349

commit v2 on v1

v2 whole, which is shorter than its diff:
```python
import functools

import jax
import jax.numpy as jnp
from jax import lax
from jax.experimental import pallas as pl
from jax.experimental.pallas import tpu as pltpu
from jax.sharding import PartitionSpec as P

MESH = pl.DeviceIdType.MESH
F32 = jnp.float32


def id_column(ids, span, lanes):
    where = lax.broadcasted_iota(jnp.int32, (span, lanes), 0)
    column = jnp.zeros((span, lanes), jnp.int32)
    for t in range(span):
        column = jnp.where(where == t, ids[t], column)
    return column


def id_row(ids, span, lanes):
    where = lax.broadcasted_iota(jnp.int32, (span, lanes), 1) % span
    row = jnp.zeros((span, lanes), jnp.int32)
    for t in range(span):
        row = jnp.where(where == t, ids[t], row)
    return row


def edge_masks(ids, span, lanes):
    column = id_column(ids, span, lanes)
    return (column == ids[0]).astype(F32), (column == ids[span - 1]).astype(F32)


def stack_rows(values, rows, lanes):
    where = lax.broadcasted_iota(jnp.int32, (rows, lanes), 0)
    tile = jnp.zeros((rows, lanes), F32)
    for i, value in enumerate(values):
        tile = jnp.where(where == i, value, tile)
    return tile


def exchange_kernel(
    n, n_prod, slices, loads, wide,
    week, month, year, x_hbm,
    carry, near, meta, mixer, gains,
    x, send1, recv1, send2, edges, seen, parts,
    load_sem, id_s, id_r, s1_sem, r1_sem, s2_sem, r2_sem, sib_s, sib_r, near_s, near_r,
):
    me = lax.axis_index("date")
    core = lax.axis_index("prod")
    columns, span, lanes = x.shape
    rows = columns // slices
    chunk = columns // loads
    last = span - 1
    loaded = [
        pltpu.make_async_copy(
            x_hbm.at[pl.ds(i * chunk, chunk)], x.at[pl.ds(i * chunk, chunk)], load_sem.at[i]
        )
        for i in range(loads)
    ]
    for copy in loaded:
        copy.start()
    barrier = pltpu.get_barrier_semaphore()
    for d in range(1, n):
        pl.semaphore_signal(
            barrier, inc=1, device_id=(lax.rem(me + d, n), core), device_id_type=MESH
        )
    for d in range(1, n_prod):
        pl.semaphore_signal(
            barrier, inc=1, device_id=(me, lax.rem(core + d, n_prod)), device_id_type=MESH
        )
    lane = lax.broadcasted_iota(jnp.int32, (1, lanes), 1)
    ids = jnp.zeros((1, lanes), F32)
    for i, v in enumerate((year[0], year[last], week[0], week[last], month[0], month[last])):
        ids = jnp.where(lane == i, v.astype(F32), ids)
    seen[me] = ids
    head_y, tail_y = edge_masks(year, span, lanes)

    def outer_sums(s, total):
        block = x[pl.ds(pl.multiple_of(s * rows, rows), rows)]
        send1[s, 0] = jnp.sum(block * head_y[None], axis=1)
        send1[s, 1] = jnp.sum(block * tail_y[None], axis=1)
        if wide:
            send1[s, 2] = jnp.sum(block, axis=1)
        return total + jnp.sum(block, axis=0)

    total = jnp.zeros((span, lanes), F32)
    per_load = slices // loads
    for i in range(loads):
        loaded[i].wait()
        total = lax.fori_loop(i * per_load, (i + 1) * per_load, outer_sums, total)
    recv1[me] = send1[lax.rem(me, slices)]
    pl.semaphore_wait(barrier, n - 1 + n_prod - 1)

    def to_all(source, target, send_sem, recv_sem):
        copies = []
        for d in range(1, n):
            peer = lax.rem(me + d, n)
            copy = pltpu.make_async_remote_copy(
                src_ref=source(peer), dst_ref=target.at[me],
                send_sem=send_sem.at[peer], recv_sem=recv_sem.at[me],
                device_id=(peer, core), device_id_type=MESH,
            )
            copy.start()
            copies.append(copy)
        return copies

    def arrived(target, send_sem, recv_sem):
        for d in range(1, n):
            peer = lax.rem(me + d, n)
            pltpu.make_async_remote_copy(
                src_ref=target.at[me], dst_ref=target.at[peer],
                send_sem=send_sem.at[peer], recv_sem=recv_sem.at[peer],
                device_id=(peer, core), device_id_type=MESH,
            ).wait_recv()

    sent = to_all(lambda peer: seen.at[me], seen, id_s, id_r)
    sent += to_all(lambda peer: send1.at[lax.rem(peer, slices)], recv1, s1_sem, r1_sem)

    left, right = lax.rem(me + n - 1, n), lax.rem(me + 1, n)

    def edge_sums(level, head, tail):
        def inner_sums(s, nothing):
            at = pl.ds(pl.multiple_of(s * rows, rows), rows)
            block = x[at]
            edges[0, level, at] = jnp.sum(block * tail[None], axis=1)
            edges[1, level, at] = jnp.sum(block * head[None], axis=1)
            return nothing

        lax.fori_loop(0, slices, inner_sums, 0)

    def edge_sends(level):
        copies = []
        for side, peer in ((0, right), (1, left)):
            copy = pltpu.make_async_remote_copy(
                src_ref=edges.at[side, level], dst_ref=near.at[side, level],
                send_sem=near_s.at[side, level], recv_sem=near_r.at[side, level],
                device_id=(peer, core), device_id_type=MESH,
            )
            copy.start()
            copies.append(copy)
        return copies

    head_w, tail_w = edge_masks(week, span, lanes)
    edge_sums(0, head_w, tail_w)
    beside = edge_sends(0)
    head_m, tail_m = edge_masks(month, span, lanes)
    edge_sums(1, head_m, tail_m)

    sub = lax.broadcasted_iota(jnp.int32, (span, 3 * span), 0)
    place = lax.broadcasted_iota(jnp.int32, (span, 3 * span), 1) % span
    mixer[0:span] = jnp.where(place <= sub, 1.0, 0.0).astype(mixer.dtype)
    for k, level in enumerate((week, month, year)):
        same = id_column(level, span, 3 * span) == id_row(level, span, 3 * span)
        mixer[(k + 1) * span : (k + 2) * span] = jnp.where(same, 1.0, 0.0).astype(mixer.dtype)

    arrived(seen, id_s, id_r)
    low = [jnp.broadcast_to(seen[b][:, 0:1], (rows, lanes)) for b in range(n)]
    top = [jnp.broadcast_to(seen[b][:, 1:2], (rows, lanes)) for b in range(n)]
    arrived(recv1, s1_sem, r1_sem)
    zero = jnp.zeros((rows, lanes), F32)
    running, into = zero, zero
    brought = []
    for b in range(n):
        send2[b, 0] = running
        brought.append(into)
        if wide:
            send2[b, 1] = into
        if b + 1 < n:
            head, tail = recv1[b, 0], recv1[b, 1]
            one = low[b] == top[b]
            running = running + (recv1[b, 2] if wide else head + jnp.where(one, 0.0, tail))
            into = jnp.where(top[b] == low[b + 1], tail + jnp.where(one, into, 0.0), 0.0)
    back = zero
    for b in reversed(range(n)):
        one = low[b] == top[b]
        if wide:
            send2[b, 2] = back
        else:
            send2[b, 1] = back + jnp.where(one, brought[b], 0.0)
        if b > 0:
            held = recv1[b, 0] + jnp.where(one, back, 0.0)
            back = jnp.where(top[b - 1] == low[b], held, 0.0)
    sent += to_all(lambda peer: send2.at[peer], carry, s2_sem, r2_sem)
    beside += edge_sends(1)
    carry[me] = send2[me]

    def gain(there, lane_seen, own, where):
        value = jnp.broadcast_to(seen[there][:, lane_seen : lane_seen + 1], (1, lanes))
        return jnp.where(jnp.logical_and(value == own.astype(F32), where), 1.0, 0.0)

    gains[0] = head_w * gain(left, 3, week[0], me > 0)
    gains[1] = tail_w * gain(right, 2, week[last], me < n - 1)
    gains[2] = head_m * gain(left, 5, month[0], me > 0)
    gains[3] = tail_m * gain(right, 4, month[last], me < n - 1)
    gains[4] = head_y if wide else head_y * jnp.where(year[0] == year[last], 0.0, 1.0)
    gains[5] = tail_y
    for copy in beside:
        copy.wait_recv()
    arrived(carry, s2_sem, r2_sem)
    kept = carry[0:slices]

    def over_products(value):
        return jnp.sum(value.reshape(columns, lanes), axis=0, keepdims=True)

    parts[core, 0:8] = stack_rows(
        [
            over_products(kept[:, 0]),
            over_products(kept[:, 1 if wide else 0]),
            over_products(kept[:, 2 if wide else 1]),
            over_products(near[0, 0]), over_products(near[0, 1]),
            over_products(near[1, 0]), over_products(near[1, 1]),
        ],
        8, lanes,
    )
    parts[core, 8 : 8 + span] = total
    shared = []
    for d in range(1, n_prod):
        peer = lax.rem(core + d, n_prod)
        copy = pltpu.make_async_remote_copy(
            src_ref=parts.at[core], dst_ref=parts.at[core],
            send_sem=sib_s.at[peer], recv_sem=sib_r.at[core],
            device_id=(me, peer), device_id_type=MESH,
        )
        copy.start()
        shared.append(copy)
    for copy in sent + beside:
        copy.wait_send()
    for d in range(1, n_prod):
        peer = lax.rem(core + d, n_prod)
        pltpu.make_async_remote_copy(
            src_ref=parts.at[core], dst_ref=parts.at[peer],
            send_sem=sib_s.at[peer], recv_sem=sib_r.at[peer],
            device_id=(me, peer), device_id_type=MESH,
        ).wait_recv()
    whole = parts[0]
    for i in range(1, n_prod):
        whole = whole + parts[i]
    meta[...] = whole
    for copy in shared:
        copy.wait_send()


def exchange(n, n_prod, slices, wide, week, month, year, sales):
    columns, span, lanes = sales.shape
    rows = columns // slices
    loads = 4 if slices % 4 == 0 else 1
    smem = pl.BlockSpec(memory_space=pltpu.SMEM)
    vmem = pl.BlockSpec(memory_space=pltpu.VMEM)
    packet = (n, 3 if wide else 2, rows, lanes)
    dma = pltpu.SemaphoreType.DMA
    return pl.pallas_call(
        functools.partial(exchange_kernel, n, n_prod, slices, loads, wide),
        out_shape=(
            jax.ShapeDtypeStruct(packet, F32),
            jax.ShapeDtypeStruct((2, 2, columns, lanes), F32),
            jax.ShapeDtypeStruct((8 + span, lanes), F32),
            jax.ShapeDtypeStruct((4 * span, 3 * span), jnp.bfloat16),
            jax.ShapeDtypeStruct((6, span, lanes), F32),
        ),
        in_specs=[smem, smem, smem, pl.BlockSpec(memory_space=pl.ANY)],
        out_specs=(vmem,) * 5,
        scratch_shapes=[
            pltpu.VMEM(sales.shape, F32),
            pltpu.VMEM((slices,) + packet[1:], F32),
            pltpu.VMEM(packet, F32),
            pltpu.VMEM(packet, F32),
            pltpu.VMEM((2, 2, columns, lanes), F32),
            pltpu.VMEM((n, 1, lanes), F32),
            pltpu.VMEM((n_prod, 8 + span, lanes), F32),
            dma((loads,)), dma((n,)), dma((n,)), dma((n,)), dma((n,)), dma((n,)), dma((n,)),
            dma((n_prod,)), dma((n_prod,)), dma((2, 2)), dma((2, 2)),
        ],
        compiler_params=pltpu.CompilerParams(collective_id=0, has_side_effects=True),
        name="exchange",
    )(week, month, year, sales)


def split3(value):
    high = value.astype(jnp.bfloat16)
    rest = value - high.astype(F32)
    middle = rest.astype(jnp.bfloat16)
    low = (rest - middle.astype(F32)).astype(jnp.bfloat16)
    return jnp.concatenate([high, middle, low], axis=-2)


def apply_kernel(
    wide, x, carry, near, meta, mixer, gains,
    run_out, week_out, month_out, year_out, rollup,
):
    _, span, lanes = x.shape
    groups, _, rows, _ = carry.shape

    @pl.when(pl.program_id(0) == 0)
    def _():
        mixed = jnp.dot(mixer[...], split3(meta[8 : 8 + span]), preferred_element_type=F32)
        rollup[0] = mixed[0:span] + meta[0:1]
        rollup[1] = mixed[span : 2 * span] + meta[3:4] * gains[0] + meta[5:6] * gains[1]
        rollup[2] = mixed[2 * span : 3 * span] + meta[4:5] * gains[2] + meta[6:7] * gains[3]
        rollup[3] = mixed[3 * span : 4 * span] + meta[1:2] * gains[4] + meta[2:3] * gains[5]

    def group(g, nothing):
        base = pl.multiple_of(g * rows, rows)
        at = pl.ds(base, rows)
        left_w, left_m = near[0, 0, at], near[0, 1, at]
        right_w, right_m = near[1, 0, at], near[1, 1, at]
        start = carry[g, 0]
        year_l, year_r = carry[g, 1 if wide else 0], carry[g, 2 if wide else 1]
        for r in range(0, rows, 2):
            parts = split3(x[pl.ds(base + r, 2)])
            both = jnp.concatenate([parts[0], parts[1]], axis=1)
            mixed = jnp.dot(mixer[...], both, preferred_element_type=F32)
            for j in range(2):
                q = r + j
                row = slice(q, q + 1)
                own = mixed[:, j * lanes : (j + 1) * lanes]
                run_out[base + q] = own[0:span] + start[row]
                week_out[base + q] = (
                    own[span : 2 * span] + left_w[row] * gains[0] + right_w[row] * gains[1]
                )
                month_out[base + q] = (
                    own[2 * span : 3 * span] + left_m[row] * gains[2] + right_m[row] * gains[3]
                )
                year_out[base + q] = (
                    own[3 * span : 4 * span] + year_l[row] * gains[4] + year_r[row] * gains[5]
                )
        return nothing

    lax.fori_loop(0, groups, group, 0, unroll=groups <= 2)


def apply(slices, wide, sales, carry, near, meta, mixer, gains):
    columns, span, lanes = sales.shape
    rows = columns // slices
    steps = 8 if slices % 8 == 0 else 1
    block = columns // steps
    cube = pl.BlockSpec((block, span, lanes), lambda i: (i, 0, 0))
    cube_shape = jax.ShapeDtypeStruct(sales.shape, F32)
    return pl.pallas_call(
        functools.partial(apply_kernel, wide),
        grid=(steps,),
        out_shape=(cube_shape,) * 4 + (jax.ShapeDtypeStruct((4, span, lanes), F32),),
        in_specs=[
            cube,
            pl.BlockSpec((slices // steps, carry.shape[1], rows, lanes), lambda i: (i, 0, 0, 0)),
            pl.BlockSpec((2, 2, block, lanes), lambda i: (0, 0, i, 0)),
            pl.BlockSpec(meta.shape, lambda i: (0, 0)),
            pl.BlockSpec(mixer.shape, lambda i: (0, 0)),
            pl.BlockSpec(gains.shape, lambda i: (0, 0, 0)),
        ],
        out_specs=(cube,) * 4 + (pl.BlockSpec((4, span, lanes), lambda i: (0, 0, 0)),),
        compiler_params=pltpu.CompilerParams(dimension_semantics=("arbitrary",)),
        name="apply",
    )(sales, carry, near, meta, mixer, gains)


def solution(mesh):
    n, n_prod = mesh.shape["date"], mesh.shape["prod"]

    def local(sales, week, month, year):
        slices = min(n, sales.shape[0] // 8)
        wide = n * sales.shape[1] // 300 + 1 > 2
        passed = exchange(n, n_prod, slices, wide, week, month, year, sales)
        return apply(slices, wide, sales, *passed)

    return jax.shard_map(
        local,
        mesh=mesh,
        in_specs=(P("prod", "date", None), P("date"), P("date"), P("date")),
        out_specs=(P("prod", "date", None),) * 4 + (P(None, "date", None),),
        check_vma=False,
    )
```

time: 35.4 us -> 33.3 us (0.941)
  Pallas kernels: 34.5 us -> 32.4 us
    pallas_call x1, Pallas kernels: 26 us -> 24.6 us  [exchange(): pl.pallas_call(functools.partial(exchange_kernel, n, n_prod, slices, load...]
    pallas_call x1, Pallas kernels: 8.48 us -> 7.77 us  [apply(): pl.pallas_call(functools.partial(apply_kernel, wide), grid=(steps,), out_...]
where the time goes in v2:
time: 33.3 us; the launch traced here: 33 us
  Pallas kernels  32.4 us (97%)
  between operations  0.64 us (2%)
    pallas_call x1, Pallas kernels, exchange(): pl.pallas_call(functools.partial(exchange_kernel, n, n_prod, slices, load...  24.6 us
    pallas_call x1, Pallas kernels, apply(): pl.pallas_call(functools.partial(apply_kernel, wide), grid=(steps,), out_...  7.77 us

profile of v2, /device:TPU:0, one launch (start us, length us, event | category | flops | bytes accessed | tf_op | source)
XLA Modules:
  0.0 33.0 jit_solution(12542839523129400461)
XLA Ops:
  0.6 24.6 %exchange.1 = (f32[16,2,8,128]{3,2,1,0:T(8,128)}, f32[2,2,128,128]{3,2,1,0:T(8,128)}, f32[40,128]{1,0:T(8,128)}, bf16[128,96]{1,0:T(8,128)(2,1)}, f32[6,32,128]{2,1,0:T(8,128)}) custom-call(s32[32]{0:T(128)} %week.1, s32[32]{0:T(128)} %month.1, s32[32]{0:T(128)} %year.1, f32[128,32,128]{2,1,0:T(8,128)} %x.1), custom_call_target="tpu_custom_call" | custom-call | tf_op jit(solution)/shard_map/exchange/pallas_call | solution.py:253
  25.3 7.8 %apply.1 = (f32[128,32,128]{2,1,0:T(8,128)}, f32[128,32,128]{2,1,0:T(8,128)}, f32[128,32,128]{2,1,0:T(8,128)}, f32[128,32,128]{2,1,0:T(8,128)}, f32[4,32,128]{2,1,0:T(8,128)}) custom-call(f32[128,32,128]{2,1,0:T(8,128)} %x.1, f32[16,2,8,128]{3,2,1,0:T(8,128)} %get-tuple-element.10.carry, f32[2,2,128,128]{3,2,1,0:T(8,128)} %get-tuple-element.11.near, ...), custom_call_target="tpu_custom_call" | custom-call | tf_op jit(solution)/shard_map/apply/pallas_call | solution.py:340

commit v3 on v2

--- a/solution.py
+++ b/solution.py
@@ -42,10 +42,11 @@
 
 def exchange_kernel(
     n, n_prod, slices, loads, wide,
-    week, month, year, x_hbm,
-    carry, near, meta, mixer, gains,
-    x, send1, recv1, send2, edges, seen, parts,
-    load_sem, id_s, id_r, s1_sem, r1_sem, s2_sem, r2_sem, sib_s, sib_r, near_s, near_r,
+    week_hbm, month_hbm, year_hbm, x_hbm,
+    carry, near, meta_hbm, mixer_hbm, gains_hbm,
+    week, month, year, meta, mixer, gains,
+    x, send1, recv1, send2, edges, seen, summed, parts,
+    ids_sem, out_sem, sum_s, sum_r, load_sem, id_s, id_r, s1_sem, r1_sem, s2_sem, r2_sem, sib_s, sib_r, near_s, near_r,
 ):
     me = lax.axis_index("date")
     core = lax.axis_index("prod")
@@ -61,6 +62,14 @@
     ]
     for copy in loaded:
         copy.start()
+    fetched = [
+        pltpu.make_async_copy(source, target, ids_sem.at[i])
+        for i, (source, target) in enumerate(
+            ((year_hbm, year), (week_hbm, week), (month_hbm, month))
+        )
+    ]
+    for copy in fetched:
+        copy.start()
     barrier = pltpu.get_barrier_semaphore()
     for d in range(1, n):
         pl.semaphore_signal(
@@ -70,6 +79,8 @@
         pl.semaphore_signal(
             barrier, inc=1, device_id=(me, lax.rem(core + d, n_prod)), device_id_type=MESH
         )
+    for copy in fetched:
+        copy.wait()
     lane = lax.broadcasted_iota(jnp.int32, (1, lanes), 1)
     ids = jnp.zeros((1, lanes), F32)
     for i, v in enumerate((year[0], year[last], week[0], week[last], month[0], month[last])):
@@ -118,6 +129,16 @@
     sent = to_all(lambda peer: seen.at[me], seen, id_s, id_r)
     sent += to_all(lambda peer: send1.at[lax.rem(peer, slices)], recv1, s1_sem, r1_sem)
 
+    head_w, tail_w = edge_masks(week, span, lanes)
+    head_m, tail_m = edge_masks(month, span, lanes)
+    summed[me] = stack_rows(
+        [jnp.sum(total, axis=0, keepdims=True)]
+        + [
+            jnp.sum(total * m, axis=0, keepdims=True)
+            for m in (head_y, tail_y, head_w, tail_w, head_m, tail_m)
+        ],
+        8, lanes,
+    )
     left, right = lax.rem(me + n - 1, n), lax.rem(me + 1, n)
 
     def edge_sums(level, head, tail):
@@ -130,23 +151,20 @@
 
         lax.fori_loop(0, slices, inner_sums, 0)
 
-    def edge_sends(level):
-        copies = []
-        for side, peer in ((0, right), (1, left)):
-            copy = pltpu.make_async_remote_copy(
-                src_ref=edges.at[side, level], dst_ref=near.at[side, level],
-                send_sem=near_s.at[side, level], recv_sem=near_r.at[side, level],
-                device_id=(peer, core), device_id_type=MESH,
-            )
-            copy.start()
-            copies.append(copy)
-        return copies
-
-    head_w, tail_w = edge_masks(week, span, lanes)
+    def edge_send(side, level):
+        copy = pltpu.make_async_remote_copy(
+            src_ref=edges.at[side, level], dst_ref=near.at[side, level],
+            send_sem=near_s.at[side, level], recv_sem=near_r.at[side, level],
+            device_id=((right, left)[side], core), device_id_type=MESH,
+        )
+        copy.start()
+        return copy
+
     edge_sums(0, head_w, tail_w)
-    beside = edge_sends(0)
-    head_m, tail_m = edge_masks(month, span, lanes)
+    sent += to_all(lambda peer: summed.at[me], summed, sum_s, sum_r)
+    beside = [edge_send(0, 0), edge_send(1, 0)]
     edge_sums(1, head_m, tail_m)
+    beside.append(edge_send(0, 1))
 
     sub = lax.broadcasted_iota(jnp.int32, (span, 3 * span), 0)
     place = lax.broadcasted_iota(jnp.int32, (span, 3 * span), 1) % span
@@ -183,8 +201,9 @@
             held = recv1[b, 0] + jnp.where(one, back, 0.0)
             back = jnp.where(top[b - 1] == low[b], held, 0.0)
     sent += to_all(lambda peer: send2.at[peer], carry, s2_sem, r2_sem)
-    beside += edge_sends(1)
-    carry[me] = send2[me]
+    beside.append(edge_send(1, 1))
+    kept = pltpu.make_async_copy(send2.at[me], carry.at[me], out_sem.at[0])
+    kept.start()
 
     def gain(there, lane_seen, own, where):
         value = jnp.broadcast_to(seen[there][:, lane_seen : lane_seen + 1], (1, lanes))
@@ -196,21 +215,36 @@
     gains[3] = tail_m * gain(right, 4, month[last], me < n - 1)
     gains[4] = head_y if wide else head_y * jnp.where(year[0] == year[last], 0.0, 1.0)
     gains[5] = tail_y
-    for copy in beside:
-        copy.wait_recv()
-    arrived(carry, s2_sem, r2_sem)
-    kept = carry[0:slices]
-
-    def over_products(value):
-        return jnp.sum(value.reshape(columns, lanes), axis=0, keepdims=True)
-
+    leaving = [
+        pltpu.make_async_copy(mixer, mixer_hbm, out_sem.at[1]),
+        pltpu.make_async_copy(gains, gains_hbm, out_sem.at[2]),
+    ]
+    for copy in leaving:
+        copy.start()
+
+    arrived(summed, sum_s, sum_r)
+    run_sum = jnp.zeros((1, lanes), F32)
+    in_sum, back_sum = run_sum, run_sum
+    low_me, top_me = low[0][0:1] * 0.0, top[0][0:1] * 0.0
+    low_me = low_me + year[0].astype(F32)
+    top_me = top_me + year[last].astype(F32)
+    for b in range(n):
+        tile = summed[b]
+        run_sum = run_sum + jnp.where(b < me, tile[0:1], 0.0)
+        inside = jnp.logical_and(top[b][0:1] == low_me, b < me)
+        in_sum = in_sum + jnp.where(inside, tile[2:3], 0.0)
+        inside = jnp.logical_and(low[b][0:1] == top_me, b > me)
+        back_sum = back_sum + jnp.where(inside, tile[1:2], 0.0)
+    if wide:
+        first_sum, last_sum = in_sum, back_sum
+    else:
+        first_sum = run_sum
+        last_sum = back_sum + jnp.where(low_me == top_me, in_sum, 0.0)
+    from_left, from_right = summed[left], summed[right]
     parts[core, 0:8] = stack_rows(
         [
-            over_products(kept[:, 0]),
-            over_products(kept[:, 1 if wide else 0]),
-            over_products(kept[:, 2 if wide else 1]),
-            over_products(near[0, 0]), over_products(near[0, 1]),
-            over_products(near[1, 0]), over_products(near[1, 1]),
+            run_sum, first_sum, last_sum,
+            from_left[4:5], from_left[6:7], from_right[3:4], from_right[5:6],
         ],
         8, lanes,
     )
@@ -225,8 +259,6 @@
         )
         copy.start()
         shared.append(copy)
-    for copy in sent + beside:
-        copy.wait_send()
     for d in range(1, n_prod):
         peer = lax.rem(core + d, n_prod)
         pltpu.make_async_remote_copy(
@@ -238,16 +270,24 @@
     for i in range(1, n_prod):
         whole = whole + parts[i]
     meta[...] = whole
-    for copy in shared:
+    last_out = pltpu.make_async_copy(meta, meta_hbm, out_sem.at[3])
+    last_out.start()
+    for copy in sent + beside + shared:
         copy.wait_send()
+    kept.wait()
+    for copy in leaving:
+        copy.wait()
+    for copy in beside:
+        copy.wait_recv()
+    arrived(carry, s2_sem, r2_sem)
+    last_out.wait()
 
 
 def exchange(n, n_prod, slices, wide, week, month, year, sales):
     columns, span, lanes = sales.shape
     rows = columns // slices
     loads = 4 if slices % 4 == 0 else 1
-    smem = pl.BlockSpec(memory_space=pltpu.SMEM)
-    vmem = pl.BlockSpec(memory_space=pltpu.VMEM)
+    anywhere = pl.BlockSpec(memory_space=pl.ANY)
     packet = (n, 3 if wide else 2, rows, lanes)
     dma = pltpu.SemaphoreType.DMA
     return pl.pallas_call(
@@ -259,17 +299,24 @@
             jax.ShapeDtypeStruct((4 * span, 3 * span), jnp.bfloat16),
             jax.ShapeDtypeStruct((6, span, lanes), F32),
         ),
-        in_specs=[smem, smem, smem, pl.BlockSpec(memory_space=pl.ANY)],
-        out_specs=(vmem,) * 5,
+        in_specs=[anywhere] * 4,
+        out_specs=(anywhere,) * 5,
         scratch_shapes=[
+            pltpu.SMEM((span,), jnp.int32),
+            pltpu.SMEM((span,), jnp.int32),
+            pltpu.SMEM((span,), jnp.int32),
+            pltpu.VMEM((8 + span, lanes), F32),
+            pltpu.VMEM((4 * span, 3 * span), jnp.bfloat16),
+            pltpu.VMEM((6, span, lanes), F32),
             pltpu.VMEM(sales.shape, F32),
             pltpu.VMEM((slices,) + packet[1:], F32),
             pltpu.VMEM(packet, F32),
             pltpu.VMEM(packet, F32),
             pltpu.VMEM((2, 2, columns, lanes), F32),
             pltpu.VMEM((n, 1, lanes), F32),
+            pltpu.VMEM((n, 8, lanes), F32),
             pltpu.VMEM((n_prod, 8 + span, lanes), F32),
-            dma((loads,)), dma((n,)), dma((n,)), dma((n,)), dma((n,)), dma((n,)), dma((n,)),
+            dma((3,)), dma((4,)), dma((n,)), dma((n,)), dma((loads,)), dma((n,)), dma((n,)), dma((n,)), dma((n,)), dma((n,)), dma((n,)),
             dma((n_prod,)), dma((n_prod,)), dma((2, 2)), dma((2, 2)),
         ],
         compiler_params=pltpu.CompilerParams(collective_id=0, has_side_effects=True),
@@ -286,19 +333,35 @@
 
 
 def apply_kernel(
-    wide, x, carry, near, meta, mixer, gains,
-    run_out, week_out, month_out, year_out, rollup,
+    wide, steps, x_hbm, carry_hbm, near_hbm, meta_hbm, mixer_hbm, gains_hbm,
+    run_hbm, week_hbm, month_hbm, year_hbm, rollup_hbm,
+    x, carry, near, meta, mixer, gains, run_out, week_out, month_out, year_out, rollup,
+    x_sem, in_sem, out_sem, rollup_sem,
 ):
-    _, span, lanes = x.shape
+    columns, span, lanes = x.shape
     groups, _, rows, _ = carry.shape
-
-    @pl.when(pl.program_id(0) == 0)
-    def _():
-        mixed = jnp.dot(mixer[...], split3(meta[8 : 8 + span]), preferred_element_type=F32)
-        rollup[0] = mixed[0:span] + meta[0:1]
-        rollup[1] = mixed[span : 2 * span] + meta[3:4] * gains[0] + meta[5:6] * gains[1]
-        rollup[2] = mixed[2 * span : 3 * span] + meta[4:5] * gains[2] + meta[6:7] * gains[3]
-        rollup[3] = mixed[3 * span : 4 * span] + meta[1:2] * gains[4] + meta[2:3] * gains[5]
+    per_step = groups // steps
+    block = columns // steps
+    small = [
+        pltpu.make_async_copy(source, target, in_sem.at[i])
+        for i, (source, target) in enumerate(
+            (
+                (mixer_hbm, mixer), (gains_hbm, gains),
+                (carry_hbm.at[pl.ds(0, groups)], carry), (near_hbm, near), (meta_hbm, meta),
+            )
+        )
+    ]
+    pieces = [pl.ds(i * block, block) for i in range(steps)]
+    loads = [
+        pltpu.make_async_copy(x_hbm.at[at], x.at[at], x_sem.at[i]) for i, at in enumerate(pieces)
+    ]
+    loads[0].start()
+    for copy in small:
+        copy.start()
+    for copy in loads[1:]:
+        copy.start()
+    for copy in small:
+        copy.wait()
 
     def group(g, nothing):
         base = pl.multiple_of(g * rows, rows)
@@ -327,30 +390,55 @@
                 )
         return nothing
 
-    lax.fori_loop(0, groups, group, 0, unroll=groups <= 2)
+    stores = []
+    for i, at in enumerate(pieces):
+        loads[i].wait()
+        lax.fori_loop(i * per_step, (i + 1) * per_step, group, 0)
+        for k, (source, target) in enumerate(
+            (
+                (run_out, run_hbm), (week_out, week_hbm),
+                (month_out, month_hbm), (year_out, year_hbm),
+            )
+        ):
+            copy = pltpu.make_async_copy(source.at[at], target.at[at], out_sem.at[i, k])
+            copy.start()
+            stores.append(copy)
+        if i == 0:
+            mixed = jnp.dot(mixer[...], split3(meta[8 : 8 + span]), preferred_element_type=F32)
+            rollup[0] = mixed[0:span] + meta[0:1]
+            rollup[1] = mixed[span : 2 * span] + meta[3:4] * gains[0] + meta[5:6] * gains[1]
+            rollup[2] = mixed[2 * span : 3 * span] + meta[4:5] * gains[2] + meta[6:7] * gains[3]
+            rollup[3] = mixed[3 * span : 4 * span] + meta[1:2] * gains[4] + meta[2:3] * gains[5]
+            copy = pltpu.make_async_copy(rollup, rollup_hbm, rollup_sem.at[0])
+            copy.start()
+            stores.append(copy)
+    for copy in stores:
+        copy.wait()
 
 
 def apply(slices, wide, sales, carry, near, meta, mixer, gains):
-    columns, span, lanes = sales.shape
-    rows = columns // slices
+    span, lanes = sales.shape[1:]
     steps = 8 if slices % 8 == 0 else 1
-    block = columns // steps
-    cube = pl.BlockSpec((block, span, lanes), lambda i: (i, 0, 0))
+    anywhere = pl.BlockSpec(memory_space=pl.ANY)
     cube_shape = jax.ShapeDtypeStruct(sales.shape, F32)
+    cube = pltpu.VMEM(sales.shape, F32)
+    dma = pltpu.SemaphoreType.DMA
     return pl.pallas_call(
-        functools.partial(apply_kernel, wide),
-        grid=(steps,),
+        functools.partial(apply_kernel, wide, steps),
         out_shape=(cube_shape,) * 4 + (jax.ShapeDtypeStruct((4, span, lanes), F32),),
-        in_specs=[
+        in_specs=[anywhere] * 6,
+        out_specs=(anywhere,) * 5,
+        scratch_shapes=[
             cube,
-            pl.BlockSpec((slices // steps, carry.shape[1], rows, lanes), lambda i: (i, 0, 0, 0)),
-            pl.BlockSpec((2, 2, block, lanes), lambda i: (0, 0, i, 0)),
-            pl.BlockSpec(meta.shape, lambda i: (0, 0)),
-            pl.BlockSpec(mixer.shape, lambda i: (0, 0)),
-            pl.BlockSpec(gains.shape, lambda i: (0, 0, 0)),
+            pltpu.VMEM((slices,) + carry.shape[1:], F32),
+            pltpu.VMEM(near.shape, F32),
+            pltpu.VMEM(meta.shape, F32),
+            pltpu.VMEM(mixer.shape, mixer.dtype),
+            pltpu.VMEM(gains.shape, F32),
+            cube, cube, cube, cube,
+            pltpu.VMEM((4, span, lanes), F32),
+            dma((steps,)), dma((5,)), dma((steps, 4)), dma((1,)),
         ],
-        out_specs=(cube,) * 4 + (pl.BlockSpec((4, span, lanes), lambda i: (0, 0, 0)),),
-        compiler_params=pltpu.CompilerParams(dimension_semantics=("arbitrary",)),
         name="apply",
     )(sales, carry, near, meta, mixer, gains)
 

time: 33.3 us -> 27 us (0.81)
  Pallas kernels: 32.4 us -> 26.2 us
    pallas_call x1, Pallas kernels: 24.6 us -> 19.7 us  [exchange(): pl.pallas_call(functools.partial(exchange_kernel, n, n_prod, slices, load...]
    pallas_call x1, Pallas kernels: 7.77 us -> 6.47 us  [apply(): pl.pallas_call(functools.partial(apply_kernel, wide, steps), out_shape=(c...]
where the time goes in v3:
time: 27 us; the launch traced here: 26.8 us
  Pallas kernels  26.2 us (97%)
  between operations  0.64 us (2%)
    pallas_call x1, Pallas kernels, exchange(): pl.pallas_call(functools.partial(exchange_kernel, n, n_prod, slices, load...  19.7 us
    pallas_call x1, Pallas kernels, apply(): pl.pallas_call(functools.partial(apply_kernel, wide, steps), out_shape=(c...  6.47 us

profile of v3, /device:TPU:0, one launch (start us, length us, event | category | flops | bytes accessed | tf_op | source)
XLA Modules:
  0.0 26.8 jit_solution(749490607640040866)
XLA Ops:
  0.6 19.7 %exchange.1 = (f32[16,2,8,128]{3,2,1,0:T(8,128)}, f32[2,2,128,128]{3,2,1,0:T(8,128)}, f32[40,128]{1,0:T(8,128)}, bf16[128,96]{1,0:T(8,128)(2,1)}, f32[6,32,128]{2,1,0:T(8,128)}) custom-call(s32[32]{0:T(128)} %week_hbm.1, s32[32]{0:T(128)} %month_hbm.1, s32[32]{0:T(128)} %year_hbm.1, f32[128,32,128]{2,1,0:T(8,128)} %x_hbm.3), custom_call_target="tpu_custom_call" | custom-call | tf_op jit(solution)/shard_map/exchange/pallas_call | solution.py:293
  20.4 6.5 %apply.1 = (f32[128,32,128]{2,1,0:T(8,128)}, f32[128,32,128]{2,1,0:T(8,128)}, f32[128,32,128]{2,1,0:T(8,128)}, f32[128,32,128]{2,1,0:T(8,128)}, f32[4,32,128]{2,1,0:T(8,128)}) custom-call(f32[128,32,128]{2,1,0:T(8,128)} %x_hbm.3, f32[16,2,8,128]{3,2,1,0:T(8,128)} %get-tuple-element.10.carry_hbm, f32[2,2,128,128]{3,2,1,0:T(8,128)} %get-tuple-element.11.near_hbm, ...), custom_call_target="tpu_custom_call" | custom-call | tf_op jit(solution)/shard_map/apply/pallas_call | solution.py:426

commit v4 on v3

--- a/solution.py
+++ b/solution.py
@@ -106,7 +106,7 @@
 
     def to_all(source, target, send_sem, recv_sem):
         copies = []
-        for d in range(1, n):
+        for d in sorted(range(1, n), key=lambda d: -min(d, n - d)):
             peer = lax.rem(me + d, n)
             copy = pltpu.make_async_remote_copy(
                 src_ref=source(peer), dst_ref=target.at[me],
@@ -151,20 +151,32 @@
 
         lax.fori_loop(0, slices, inner_sums, 0)
 
-    def edge_send(side, level):
-        copy = pltpu.make_async_remote_copy(
+    linked = (me < n - 1, me > 0)
+
+    def edge_copy(side, level):
+        return pltpu.make_async_remote_copy(
             src_ref=edges.at[side, level], dst_ref=near.at[side, level],
             send_sem=near_s.at[side, level], recv_sem=near_r.at[side, level],
             device_id=((right, left)[side], core), device_id_type=MESH,
         )
-        copy.start()
-        return copy
+
+    def edge_send(side, level):
+        @pl.when(linked[side])
+        def _():
+            edge_copy(side, level).start()
+
+        @pl.when(jnp.logical_not(linked[side]))
+        def _():
+            pltpu.make_async_copy(
+                edges.at[side, level], near.at[1 - side, level], near_r.at[1 - side, level]
+            ).start()
 
     edge_sums(0, head_w, tail_w)
     sent += to_all(lambda peer: summed.at[me], summed, sum_s, sum_r)
-    beside = [edge_send(0, 0), edge_send(1, 0)]
+    edge_send(0, 0)
+    edge_send(1, 0)
     edge_sums(1, head_m, tail_m)
-    beside.append(edge_send(0, 1))
+    edge_send(0, 1)
 
     sub = lax.broadcasted_iota(jnp.int32, (span, 3 * span), 0)
     place = lax.broadcasted_iota(jnp.int32, (span, 3 * span), 1) % span
@@ -201,7 +213,7 @@
             held = recv1[b, 0] + jnp.where(one, back, 0.0)
             back = jnp.where(top[b - 1] == low[b], held, 0.0)
     sent += to_all(lambda peer: send2.at[peer], carry, s2_sem, r2_sem)
-    beside.append(edge_send(1, 1))
+    edge_send(1, 1)
     kept = pltpu.make_async_copy(send2.at[me], carry.at[me], out_sem.at[0])
     kept.start()
 
@@ -272,13 +284,19 @@
     meta[...] = whole
     last_out = pltpu.make_async_copy(meta, meta_hbm, out_sem.at[3])
     last_out.start()
-    for copy in sent + beside + shared:
+    for copy in sent + shared:
         copy.wait_send()
     kept.wait()
     for copy in leaving:
         copy.wait()
-    for copy in beside:
-        copy.wait_recv()
+    for side in range(2):
+        for level in range(2):
+            edge_copy(side, level).wait_recv()
+
+            @pl.when(linked[side])
+            def _():
+                edge_copy(side, level).wait_send()
+
     arrived(carry, s2_sem, r2_sem)
     last_out.wait()
 
@@ -393,7 +411,7 @@
     stores = []
     for i, at in enumerate(pieces):
         loads[i].wait()
-        lax.fori_loop(i * per_step, (i + 1) * per_step, group, 0)
+        lax.fori_loop(i * per_step, (i + 1) * per_step, group, 0, unroll=per_step <= 2)
         for k, (source, target) in enumerate(
             (
                 (run_out, run_hbm), (week_out, week_hbm),

time: 27 us -> 26.2 us (0.970)
  Pallas kernels: 26.2 us -> 25.4 us
    pallas_call x1, Pallas kernels: 6.47 us -> 5.46 us  [apply(): pl.pallas_call(functools.partial(apply_kernel, wide, steps), out_shape=(c...]
where the time goes in v4:
time: 26.2 us; the launch traced here: 26 us
  Pallas kernels  25.4 us (97%)
  between operations  0.64 us (2%)
    pallas_call x1, Pallas kernels, exchange(): pl.pallas_call(functools.partial(exchange_kernel, n, n_prod, slices, load...  19.9 us
    pallas_call x1, Pallas kernels, apply(): pl.pallas_call(functools.partial(apply_kernel, wide, steps), out_shape=(c...  5.46 us

profile of v4, /device:TPU:0, one launch (start us, length us, event | category | flops | bytes accessed | tf_op | source)
XLA Modules:
  0.0 26.0 jit_solution(2632231163322844350)
XLA Ops:
  0.6 19.9 %exchange.1 = (f32[16,2,8,128]{3,2,1,0:T(8,128)}, f32[2,2,128,128]{3,2,1,0:T(8,128)}, f32[40,128]{1,0:T(8,128)}, bf16[128,96]{1,0:T(8,128)(2,1)}, f32[6,32,128]{2,1,0:T(8,128)}) custom-call(s32[32]{0:T(128)} %week_hbm.1, s32[32]{0:T(128)} %month_hbm.1, s32[32]{0:T(128)} %year_hbm.1, f32[128,32,128]{2,1,0:T(8,128)} %x_hbm.3), custom_call_target="tpu_custom_call" | custom-call | tf_op jit(solution)/shard_map/exchange/pallas_call | solution.py:311
  20.5 5.5 %apply.1 = (f32[128,32,128]{2,1,0:T(8,128)}, f32[128,32,128]{2,1,0:T(8,128)}, f32[128,32,128]{2,1,0:T(8,128)}, f32[128,32,128]{2,1,0:T(8,128)}, f32[4,32,128]{2,1,0:T(8,128)}) custom-call(f32[128,32,128]{2,1,0:T(8,128)} %x_hbm.3, f32[16,2,8,128]{3,2,1,0:T(8,128)} %get-tuple-element.10.carry_hbm, f32[2,2,128,128]{3,2,1,0:T(8,128)} %get-tuple-element.11.near_hbm, ...), custom_call_target="tpu_custom_call" | custom-call | tf_op jit(solution)/shard_map/apply/pallas_call | solution.py:444
